TPU v7x, 32 devices: a whole 2x2x4 slice. The times are simulated.
32 devices in a mesh: vox: 16 (over z, x, core), subj: 2 (over y).
Axes of the slice: x: 2, y: 2, z: 4, core: 2. Of those that a mesh axis runs over, the one named last changes fastest.
Arguments:
- series: bfloat16 [8, 4096, 512], P('subj', 'vox'), may hold values from -6 to 6
- live_mask: int32 [4096], P('vox'), may hold values from 0 to 1, as said below
- neighbours: int32 [4096, 13], P('vox'), may hold values from -1 to 510, as said below
- start_vectors: float32 [4096, 64], P('vox'), may hold values from -60 to 60
Outputs:
- embedding: float32 [4096, 64], P('vox')
Inputs may be any that keep to these rules, and one draw needn't show every extreme that they name: `live_mask`: within each aligned block of 128 voxel slots the live slots are a leading run of 1 to 128 slots. `neighbours`: slot n of voxel i names voxel (i // 256 - 1) * 256 + n, which is live and lies before i; the entries of a row are distinct or -1; rows of dead voxels are all -1; rows of the first 256 voxels name no slot under 256.
All inputs are finite; a program needn't handle non-finite values.
Results may differ from a plain program's by a relative error of at most 0.0024.
Values may be sent and summed in bfloat16 or wider, within the bound.
No kernel may reach another device: no remote copies, remote signals or barrier semaphores. Data moves between devices by JAX's collectives and lax.ppermute only.
A program may use at most 64 MiB of HBM per device.

v0:
```python
import math
import jax
import jax.numpy as jnp
from jax import lax
from jax.sharding import PartitionSpec as P

ITERS = 3


def shifted(shard, axis, by):
    count = lax.axis_size(axis)
    pairs = [(i, i + by) for i in range(count) if 0 <= i + by < count]
    return lax.ppermute(shard, axis, pairs)


def as_sent(shard):
    return jax.tree.map(lambda a: a.astype(jnp.bfloat16) if a.dtype == jnp.float32 else a, shard)


def standard(block):
    values = block.astype(jnp.float32)
    center = values - jnp.mean(values, axis=-1, keepdims=True)
    spread = jnp.mean(center * center, axis=-1, keepdims=True)
    return (center * lax.rsqrt(spread + 1e-05)).astype(jnp.bfloat16)


def orthonormal(images):
    gram_matrix = jnp.dot(images.T, images, precision=lax.Precision.HIGHEST)
    gram_matrix = lax.psum(gram_matrix, "vox")
    factor = jnp.linalg.cholesky(gram_matrix)
    return lax.linalg.triangular_solve(
        factor, images, left_side=False, lower=True, transpose_a=True
    )


def dense_graph(weight, slots, columns_total):
    column_ids = jnp.arange(columns_total, dtype=jnp.int32)
    matrix = jnp.zeros((weight.shape[0], columns_total), jnp.float32)
    for offset in range(weight.shape[1]):
        hits = (slots[:, offset][:, None] == column_ids[None, :]).astype(jnp.float32)
        matrix = matrix + weight[:, offset][:, None] * hits
    return matrix


def product(left, right):
    return jnp.dot(left, right, precision=lax.Precision.HIGHEST)


def on_device(series, live_mask, neighbours, start_vectors):
    voxels_here = series.shape[1]
    frames = series.shape[2]
    subjects = series.shape[0] * lax.axis_size("subj")
    scale_factor = 0.5 / math.sqrt(frames * subjects)
    zscored = standard(series)
    earlier = shifted(zscored, "vox", 1)
    window = jnp.concatenate([earlier, zscored], axis=1)
    present = neighbours >= 0
    safe_slots = jnp.maximum(neighbours, 0)
    columns = []
    for offset in range(neighbours.shape[1]):
        picked = jnp.take(window, safe_slots[:, offset], axis=1)
        columns.append(
            jnp.einsum("svf,svf->v", zscored, picked, preferred_element_type=jnp.float32)
        )
    partial_sums = jnp.stack(columns, axis=1)
    summed = lax.psum(partial_sums, "subj")
    weight = jnp.where(present, jnp.exp(scale_factor * summed), 0.0)
    living = live_mask.astype(jnp.float32)
    local_graph = dense_graph(weight, neighbours, 2 * voxels_here)
    owed = jnp.sum(local_graph, axis=0)
    received = shifted(owed[:voxels_here], "vox", -1)
    degree = 1.0 + jnp.sum(weight, axis=1) + owed[voxels_here:] + received
    scaling = living * lax.rsqrt(degree)
    vectors = living[:, None] * start_vectors
    for repeat in range(ITERS):
        scaled = scaling[:, None] * vectors
        earlier_rows = shifted(as_sent(scaled), "vox", 1).astype(scaled.dtype)
        window_rows = jnp.concatenate([earlier_rows, scaled], axis=0)
        forward = product(local_graph, window_rows)
        returns = product(local_graph.T, scaled)
        arrived = shifted(as_sent(returns[:voxels_here]), "vox", -1)
        images = 0.5 * (
            vectors + scaling[:, None] * (scaled + forward + returns[voxels_here:] + arrived)
        )
        vectors = orthonormal(images)
    return vectors


def solution(mesh):
    placed = (P("subj", "vox", None), P("vox"), P("vox", None), P("vox", None))
    return jax.shard_map(
        on_device, mesh=mesh, in_specs=placed, out_specs=P("vox", None), check_vma=False
    )
```

profile of v0, /device:TPU:0, one launch (start us, length us, event | category | flops | bytes accessed | tf_op | source)
XLA Modules:
  0.0 326.5 jit_solution(9285607745963571878)
XLA Ops:
  0.0 2.1 convert_reduce_fusion
  2.2 1.2 fusion.2
  3.4 1.6 fusion.3
  5.0 2.6 collective-permute-start
  7.8 0.5 compare_and_fusion.8
  8.6 0.5 compare_and_fusion.2
  9.1 0.5 compare_and_fusion.4
  9.6 0.6 compare_and_fusion.6
  10.2 1.4 pad_maximum_fusion
  11.6 2.5 gather_fusion.3
  14.0 2.5 gather_fusion.2
  16.5 2.5 gather_fusion.1
  19.0 2.4 gather_fusion
  21.5 2.5 gather_fusion.12
  24.0 2.5 gather_fusion.11
  26.5 2.5 gather_fusion.10
  28.9 2.4 gather_fusion.9
  31.4 2.5 gather_fusion.8
  33.9 2.5 gather_fusion.7
  36.4 2.7 gather_fusion.6
  39.1 2.5 gather_fusion.5
  41.5 2.5 gather_fusion.4
  44.1 9.5 %fusion.7 = (f32[256]{0:T(256)S(1)}, f32[256]{0:T(256)S(1)}, f32[256]{0:T(256)S(1)}, f32[256]{0:T(256)S(1)}) fusion(bf16[256,4,512]{2,1,0:T(4,128)(2,1)} %gather_fusion.3, pred[256]{0:T(512)(128)(4,1)S(1)} %get-tuple-element.72, bf16[256,4,512]{2,1,0:T(4,128)(2,1)} %gather_fusion.2, pred[256]{0:T(512)(128)(4,1)S(1)} %get-tuple-element.73, ...), kind=kLoop, calls=%fused_computation.35 | loop fusion | flops 11009024 | bytes 5256192 | tf_op jit(solution)/shard_map/svf,svf->v/dot_general | solution.py:63
  53.7 14.7 %fusion.16 = (f32[256]{0:T(256)S(1)}, f32[256]{0:T(256)S(1)}, f32[256]{0:T(256)S(1)}, f32[256]{0:T(256)S(1)}, f32[256]{0:T(256)S(1)}, /*index=5*/f32[256]{0:T(25...) fusion(bf16[256,4,512]{2,1,0:T(4,128)(2,1)S(1)} %copy-done.1, pred[256]{0:T(512)(128)(4,1)S(1)} %get-tuple-element.76, ...), kind=kLoop, calls=%fused_computation.44 | loop fusion | flops 21493504 | bytes 10505472 | tf_op jit(solution)/shard_map/svf,svf->v/dot_general | solution.py:63
  68.5 9.0 %psum.28 = f32[256,13]{0,1:T(8,128)S(1)} all-reduce(f32[256,13]{0,1:T(8,128)S(1)} %stack.55), channel_id=1, replica_groups=mesh['vox'=16,'subj'=2] {'subj'}, use_global_device_ids=true, to_apply=%region_2.0 | all-reduce | flops 3328 | bytes 26624 | tf_op jit(solution)/shard_map/psum | solution.py:66
  77.5 1.0 fusion.61
  78.5 1.3 collective-permute-start.1
  79.8 9.8 %collective-permute-done.1 = f32[256]{0:T(256)S(1)} collective-permute-done((f32[256]{0:T(256)S(1)}, f32[256]{0:T(256)S(1)}, u32[]{:S(2)}, u32[]{:S(2)}) %collective-permute-start.1) | collective-permute-done | bytes 1056 | tf_op jit(solution)/shard_map/ppermute | solution.py:13
  89.6 7.1 %collective-permute-start.2 = (bf16[256,64]{0,1:T(8,128)(2,1)S(1)}, bf16[256,64]{0,1:T(8,128)(2,1)S(1)}, u32[]{:S(2)}, u32[]{:S(2)}) collective-permute-start(bf16[256,64]{0,1:T(8,128)(2,1)S(1)} %get-tuple-element.25), channel_id=1, source_target_pairs={{0,2},{2,4},{4,6},{6,8},{8,10},{10,12},{12,14},{14,16},{16,18},{18... | collective-permute-start | bytes 98312 | tf_op jit(solution)/shard_map/ppermute | solution.py:13
  96.7 0.5 fusion.65
  97.1 1.3 collective-permute-start.3
  98.5 1.8 collective-permute-done.3
  100.3 0.6 fusion.31
  100.9 0.2 fusion.66
  101.1 60.4 %psum.29 = f32[64,64]{0,1:T(8,128)S(1)} all-reduce(f32[64,64]{0,1:T(8,128)S(1)} %fusion.66), channel_id=1, replica_groups=mesh['vox'=16,'subj'=2] {'vox'}, use_global_device_ids=true, to_apply=%region_5.7 | all-reduce | flops 4096 | bytes 32768 | tf_op jit(solution)/shard_map/psum | solution.py:29
  161.6 5.8 %cholesky.59 = f32[64,64]{1,0:T(8,128)S(1)} custom-call(f32[64,64]{1,0:T(8,128)S(1)} %fusion.49), custom_call_target="Cholesky" | custom-call | tf_op jit(solution)/shard_map/jit(cholesky)/cholesky | solution.py:30
  167.5 0.6 compare_reduce_fusion.2
  168.1 0.7 fusion.41
  168.8 4.9 %custom-call.7 = f32[1,64,64]{1,2,0:T(8,128)S(1)} custom-call(f32[1,64,64]{2,1,0:T(8,128)S(1)} %fusion.41), custom_call_target="InvertDiagBlocksLowerTriangular" | custom-call | tf_op jit(solution)/shard_map/triangular_solve/custom-call.0 | solution.py:31
  173.7 0.3 fusion.58
  174.0 1.3 collective-permute-start.4
  175.3 0.5 fusion.67
  175.7 1.3 collective-permute-start.5
  177.1 1.8 collective-permute-done.5
  178.8 0.6 fusion.26
  179.5 0.2 fusion.68
  179.7 57.9 %psum.30 = f32[64,64]{0,1:T(8,128)S(1)} all-reduce(f32[64,64]{0,1:T(8,128)S(1)} %fusion.68), channel_id=1, replica_groups=mesh['vox'=16,'subj'=2] {'vox'}, use_global_device_ids=true, to_apply=%region_8.12 | all-reduce | flops 4096 | bytes 32768 | tf_op jit(solution)/shard_map/psum | solution.py:29
  237.6 5.8 %cholesky.70 = f32[64,64]{1,0:T(8,128)S(1)} custom-call(f32[64,64]{1,0:T(8,128)S(1)} %fusion.47), custom_call_target="Cholesky" | custom-call | tf_op jit(solution)/shard_map/jit(cholesky)/cholesky | solution.py:30
  243.5 0.6 compare_reduce_fusion.1
  244.2 0.7 fusion.42
  244.8 4.9 %custom-call.8 = f32[1,64,64]{1,2,0:T(8,128)S(1)} custom-call(f32[1,64,64]{2,1,0:T(8,128)S(1)} %fusion.42), custom_call_target="InvertDiagBlocksLowerTriangular" | custom-call | tf_op jit(solution)/shard_map/triangular_solve/custom-call.0 | solution.py:31
  249.7 0.3 fusion.57
  250.0 1.3 collective-permute-start.6
  251.3 0.5 fusion.69
  251.8 1.3 collective-permute-start.7
  253.1 1.8 collective-permute-done.7
  254.9 0.6 fusion.21
  255.5 0.2 fusion.70
  255.7 57.7 %psum.31 = f32[64,64]{0,1:T(8,128)S(1)} all-reduce(f32[64,64]{0,1:T(8,128)S(1)} %fusion.70), channel_id=1, replica_groups=mesh['vox'=16,'subj'=2] {'vox'}, use_global_device_ids=true, to_apply=%region_9.13 | all-reduce | flops 4096 | bytes 32768 | tf_op jit(solution)/shard_map/psum | solution.py:29
  313.6 5.8 %cholesky.81 = f32[64,64]{1,0:T(8,128)S(1)} custom-call(f32[64,64]{1,0:T(8,128)S(1)} %fusion.45), custom_call_target="Cholesky" | custom-call | tf_op jit(solution)/shard_map/jit(cholesky)/cholesky | solution.py:30
  319.4 0.6 compare_reduce_fusion
  320.1 0.7 fusion.43
  320.7 4.9 %custom-call.9 = f32[1,64,64]{1,2,0:T(8,128)S(1)} custom-call(f32[1,64,64]{2,1,0:T(8,128)S(1)} %fusion.43), custom_call_target="InvertDiagBlocksLowerTriangular" | custom-call | tf_op jit(solution)/shard_map/triangular_solve/custom-call.0 | solution.py:31
  325.6 0.9 convolution_bitcast_fusion
  (92 shorter events, 0.8 us)
Async XLA Ops:
  0.0 2.2 copy-start
  2.1 5.5 %copy-start.7 = (s32[256,13]{0,1:T(8,128)S(1)}, s32[256,13]{0,1:T(8,128)}, u32[]{:S(2)}) copy-start(s32[256,13]{0,1:T(8,128)} %param.11) | copy-start | bytes 39940
  5.0 5.2 %collective-permute-start = (bf16[4,256,512]{2,0,1:T(4,128)(2,1)S(1)}, bf16[4,256,512]{2,0,1:T(4,128)(2,1)S(1)}, u32[]{:S(2)}, u32[]{:S(2)}) collective-permute-start(bf16[4,256,512]{2,0,1:T(4,128)(2,1)S(1)} %fusion.3), channel_id=1, source_target_pairs={{0,2},{2,4},{4,6},{6,8},{8,10},{10,12},{12,14},{14,16},{16,18},{18... | collective-permute-start | bytes 3145736 | tf_op jit(solution)/shard_map/ppermute | solution.py:13
  44.0 9.6 %copy-start.1 = (bf16[256,4,512]{2,1,0:T(4,128)(2,1)S(1)}, bf16[256,4,512]{2,1,0:T(4,128)(2,1)}, u32[]{:S(2)}) copy-start(bf16[256,4,512]{2,1,0:T(4,128)(2,1)} %gather_fusion.12) | copy-start | bytes 3145732
  44.0 9.6 %copy-start.2 = (bf16[256,4,512]{2,1,0:T(4,128)(2,1)S(1)}, bf16[256,4,512]{2,1,0:T(4,128)(2,1)}, u32[]{:S(2)}) copy-start(bf16[256,4,512]{2,1,0:T(4,128)(2,1)} %gather_fusion.11) | copy-start | bytes 3145732
  44.0 9.6 %copy-start.3 = (bf16[256,4,512]{2,1,0:T(4,128)(2,1)S(1)}, bf16[256,4,512]{2,1,0:T(4,128)(2,1)}, u32[]{:S(2)}) copy-start(bf16[256,4,512]{2,1,0:T(4,128)(2,1)} %gather_fusion.10) | copy-start | bytes 3145732
  44.0 9.6 %copy-start.4 = (bf16[256,4,512]{2,1,0:T(4,128)(2,1)S(1)}, bf16[256,4,512]{2,1,0:T(4,128)(2,1)}, u32[]{:S(2)}) copy-start(bf16[256,4,512]{2,1,0:T(4,128)(2,1)} %gather_fusion.9) | copy-start | bytes 3145732
  44.0 9.6 %copy-start.5 = (bf16[256,4,512]{2,1,0:T(4,128)(2,1)S(1)}, bf16[256,4,512]{2,1,0:T(4,128)(2,1)}, u32[]{:S(2)}) copy-start(bf16[256,4,512]{2,1,0:T(4,128)(2,1)} %gather_fusion.8) | copy-start | bytes 3145732
  44.0 9.6 %copy-start.9 = (pred[256]{0:T(512)(128)(4,1)S(1)}, pred[256]{0:T(512)(128)(4,1)}, u32[]{:S(2)}) copy-start(pred[256]{0:T(512)(128)(4,1)} %get-tuple-element.78) | copy-start | bytes 772
  44.0 9.6 %copy-start.10 = (pred[256]{0:T(512)(128)(4,1)S(1)}, pred[256]{0:T(512)(128)(4,1)}, u32[]{:S(2)}) copy-start(pred[256]{0:T(512)(128)(4,1)} %get-tuple-element.79) | copy-start | bytes 772
  44.0 9.6 %copy-start.11 = (pred[256]{0:T(512)(128)(4,1)S(1)}, pred[256]{0:T(512)(128)(4,1)}, u32[]{:S(2)}) copy-start(pred[256]{0:T(512)(128)(4,1)} %get-tuple-element.80) | copy-start | bytes 772
  44.1 9.6 %copy-start.12 = (pred[256]{0:T(512)(128)(4,1)S(1)}, pred[256]{0:T(512)(128)(4,1)}, u32[]{:S(2)}) copy-start(pred[256]{0:T(512)(128)(4,1)} %get-tuple-element.81) | copy-start | bytes 772
  44.1 9.6 %copy-start.13 = (pred[256]{0:T(512)(128)(4,1)S(1)}, pred[256]{0:T(512)(128)(4,1)}, u32[]{:S(2)}) copy-start(pred[256]{0:T(512)(128)(4,1)} %get-tuple-element.82) | copy-start | bytes 772
  44.1 9.6 %copy-start.14 = (pred[256]{0:T(512)(128)(4,1)S(1)}, pred[256]{0:T(512)(128)(4,1)}, u32[]{:S(2)}) copy-start(pred[256]{0:T(512)(128)(4,1)} %get-tuple-element.83) | copy-start | bytes 772
  44.1 9.6 %copy-start.15 = (pred[256]{0:T(512)(128)(4,1)S(1)}, pred[256]{0:T(512)(128)(4,1)}, u32[]{:S(2)}) copy-start(pred[256]{0:T(512)(128)(4,1)} %compare_and_fusion.8) | copy-start | bytes 772
  53.7 26.1 %copy-start.8 = (s32[256]{0:T(256)S(1)}, s32[256]{0:T(256)}, u32[]{:S(2)}) copy-start(s32[256]{0:T(256)} %param.10) | copy-start | bytes 3076
  53.7 35.9 %copy-start.6 = (f32[256,64]{0,1:T(8,128)S(1)}, f32[256,64]{0,1:T(8,128)}, u32[]{:S(2)}) copy-start(f32[256,64]{0,1:T(8,128)} %param.12) | copy-start | bytes 196612
  78.5 11.1 %collective-permute-start.1 = (f32[256]{0:T(256)S(1)}, f32[256]{0:T(256)S(1)}, u32[]{:S(2)}, u32[]{:S(2)}) collective-permute-start(f32[256]{0:T(256)S(1)} %slice.190), channel_id=1, source_target_pairs={{2,0},{4,2},{6,4},{8,6},{10,8},{12,10},{14,12},{16,14},{18,16},{20... | collective-permute-start | bytes 3080 | tf_op jit(solution)/shard_map/ppermute | solution.py:13
  89.6 8.8 %collective-permute-start.2 = (bf16[256,64]{0,1:T(8,128)(2,1)S(1)}, bf16[256,64]{0,1:T(8,128)(2,1)S(1)}, u32[]{:S(2)}, u32[]{:S(2)}) collective-permute-start(bf16[256,64]{0,1:T(8,128)(2,1)S(1)} %get-tuple-element.25), channel_id=1, source_target_pairs={{0,2},{2,4},{4,6},{6,8},{8,10},{10,12},{12,14},{14,16},{16,18},{18... | collective-permute-start | bytes 98312 | tf_op jit(solution)/shard_map/ppermute | solution.py:13
  97.1 3.1 collective-permute-start.3
  174.0 3.1 collective-permute-start.4
  175.7 3.1 collective-permute-start.5
  250.0 3.1 collective-permute-start.6
  251.8 3.1 collective-permute-start.7
where the time goes:
time: 327 us
  blocking collectives  185 us (57%)
  other arithmetic  70 us (21%)
  local copies, waits for them, and re-layouts  32.8 us (10%)
  starting transfers between devices  17.5 us (5%)
  waiting for transfers between devices  15.1 us (5%)
  matrix products  5.26 us (2%)
    psum x3, blocking collectives, orthonormal(): gram_matrix = lax.psum(gram_matrix, 'vox')  176 us
    gather x13, local copies, waits for them, and re-layouts, on_device(): picked = jnp.take(window, safe_slots[:, offset], axis=1)  32.4 us
    dot_general x2, other arithmetic, on_device(): jnp.einsum('svf,svf->v', zscored, picked, preferred_element_type=jnp.floa...  24.1 us
    another operation x9, other arithmetic, orthonormal(): factor = jnp.linalg.cholesky(gram_matrix)  19.6 us
    ppermute x8, starting transfers between devices, shifted(): return lax.ppermute(shard, axis, pairs)  17.5 us
    another operation x6, other arithmetic, orthonormal(): lax.linalg.triangular_solve(factor, images, left_side=False, lower=True,...  16.6 us
    ppermute x8, waiting for transfers between devices, shifted(): return lax.ppermute(shard, axis, pairs)  15.1 us
    psum x1, blocking collectives, on_device(): summed = lax.psum(partial_sums, 'subj')  8.99 us
  transfers between devices with their start and end apart: 8, of which 4 were waited for; matrix products, arithmetic and copies ran while one was open for 1% of the time, Pallas kernels for 0%

commit v1 on v0

--- a/solution.py
+++ b/solution.py
@@ -5,6 +5,15 @@
 from jax.sharding import PartitionSpec as P
 
 ITERS = 3
+
+
+def add_in_pairs(array, mesh_axis):
+    count = lax.axis_size(mesh_axis)
+    total, reach = (array, 1)
+    while reach < count:
+        total = total + lax.ppermute(total, mesh_axis, [(i, i ^ reach) for i in range(count)])
+        reach = 2 * reach
+    return total
 
 
 def shifted(shard, axis, by):
@@ -26,7 +35,7 @@
 
 def orthonormal(images):
     gram_matrix = jnp.dot(images.T, images, precision=lax.Precision.HIGHEST)
-    gram_matrix = lax.psum(gram_matrix, "vox")
+    gram_matrix = add_in_pairs(gram_matrix, "vox")
     factor = jnp.linalg.cholesky(gram_matrix)
     return lax.linalg.triangular_solve(
         factor, images, left_side=False, lower=True, transpose_a=True

time: 327 us -> 205 us (0.63)
  blocking collectives: 185 us -> 8.99 us
  starting transfers between devices: 17.5 us -> 44.7 us
  waiting for transfers between devices: 15.1 us -> 41.8 us
    psum x3 -> x0, blocking collectives: 176 us -> none  [orthonormal(): gram_matrix = lax.psum(gram_matrix, 'vox')]
    ppermute x0 -> x12, starting transfers between devices: none -> 27 us  [add_in_pairs(): lax.ppermute(total, mesh_axis, [(i, i ^ reach) for i in range(count)])]
    ppermute x0 -> x12, waiting for transfers between devices: none -> 22.4 us  [add_in_pairs(): lax.ppermute(total, mesh_axis, [(i, i ^ reach) for i in range(count)])]
    ppermute x8, waiting for transfers between devices: 15.1 us -> 19.4 us  [shifted(): return lax.ppermute(shard, axis, pairs)]
  transfers between devices with their start and end apart: 8 -> 20, of which waited for: 4 -> 16; matrix products, arithmetic and copies ran while one was open for 1% -> 2% of each run, Pallas kernels for 0% -> 0%
where the time goes in v1:
time: 205 us; the launch traced here: 204 us
  other arithmetic  70.1 us (34%)
  starting transfers between devices  44.7 us (22%)
  waiting for transfers between devices  41.8 us (20%)
  local copies, waits for them, and re-layouts  32.8 us (16%)
  blocking collectives  8.99 us (4%)
  matrix products  5.27 us (3%)
    gather x13, local copies, waits for them, and re-layouts, on_device(): picked = jnp.take(window, safe_slots[:, offset], axis=1)  32.4 us
    ppermute x12, starting transfers between devices, add_in_pairs(): lax.ppermute(total, mesh_axis, [(i, i ^ reach) for i in range(count)])  27 us
    dot_general x2, other arithmetic, on_device(): jnp.einsum('svf,svf->v', zscored, picked, preferred_element_type=jnp.floa...  24.1 us
    ppermute x12, waiting for transfers between devices, add_in_pairs(): lax.ppermute(total, mesh_axis, [(i, i ^ reach) for i in range(count)])  22.4 us
    another operation x9, other arithmetic, orthonormal(): factor = jnp.linalg.cholesky(gram_matrix)  19.6 us
    ppermute x8, waiting for transfers between devices, shifted(): return lax.ppermute(shard, axis, pairs)  19.4 us
    ppermute x8, starting transfers between devices, shifted(): return lax.ppermute(shard, axis, pairs)  17.7 us
    another operation x6, other arithmetic, orthonormal(): lax.linalg.triangular_solve(factor, images, left_side=False, lower=True,...  16.6 us
  transfers between devices with their start and end apart: 20, of which 16 were waited for; matrix products, arithmetic and copies ran while one was open for 2% of the time, Pallas kernels for 0%

profile of v1, /device:TPU:0, one launch (start us, length us, event | category | flops | bytes accessed | tf_op | source)
XLA Modules:
  0.0 204.5 jit_solution(17120000626724618931)
XLA Ops:
  0.0 2.1 %convert_reduce_fusion = f32[4,256]{0,1:T(8,128)S(1)} fusion(bf16[4,256,512]{2,1,0:T(8,128)(2,1)} %param.9), kind=kLoop, calls=%fused_computation.27 | loop fusion | flops 1047552 | bytes 1052672 | tf_op jit(solution)/shard_map/reduce_sum | solution.py:31
  2.2 1.2 fusion.2
  3.4 1.6 fusion.3
  5.0 2.6 %collective-permute-start = (bf16[4,256,512]{2,0,1:T(4,128)(2,1)S(1)}, bf16[4,256,512]{2,0,1:T(4,128)(2,1)S(1)}, u32[]{:S(2)}, u32[]{:S(2)}) collective-permute-start(bf16[4,256,512]{2,0,1:T(4,128)(2,1)S(1)} %fusion.3), channel_id=1, source_target_pairs={{0,2},{2,4},{4,6},{6,8},{8,10},{10,12},{12,14},{14,16},{16,18},{18... | collective-permute-start | bytes 3145736 | tf_op jit(solution)/shard_map/ppermute | solution.py:22
  10.2 1.4 pad_maximum_fusion
  11.6 2.5 %gather_fusion.3 = bf16[256,4,512]{2,1,0:T(4,128)(2,1)} fusion(bf16[4,512,512]{2,0,1:T(4,128)(2,1)S(1)} %pad_maximum_fusion, s32[1024]{0:T(1024)S(1)} %pad_clamp_fusion.9), kind=kCustom, calls=%fused_computation.3.clone | custom fusion | bytes 2098176 | tf_op jit(solution)/shard_map/jit(_take)/gather | solution.py:70
  14.0 2.5 %gather_fusion.2 = bf16[256,4,512]{2,1,0:T(4,128)(2,1)} fusion(bf16[4,512,512]{2,0,1:T(4,128)(2,1)S(1)} %pad_maximum_fusion, s32[1024]{0:T(1024)S(1)} %pad_clamp_fusion.10), kind=kCustom, calls=%fused_computation.2.clone | custom fusion | bytes 2098176 | tf_op jit(solution)/shard_map/jit(_take)/gather | solution.py:70
  16.5 2.5 %gather_fusion.1 = bf16[256,4,512]{2,1,0:T(4,128)(2,1)} fusion(bf16[4,512,512]{2,0,1:T(4,128)(2,1)S(1)} %pad_maximum_fusion, s32[1024]{0:T(1024)S(1)} %pad_clamp_fusion.11), kind=kCustom, calls=%fused_computation.1.clone | custom fusion | bytes 2098176 | tf_op jit(solution)/shard_map/jit(_take)/gather | solution.py:70
  19.0 2.4 %gather_fusion = bf16[256,4,512]{2,1,0:T(4,128)(2,1)} fusion(bf16[4,512,512]{2,0,1:T(4,128)(2,1)S(1)} %pad_maximum_fusion, s32[1024]{0:T(1024)S(1)} %pad_clamp_fusion.12), kind=kCustom, calls=%fused_computation.clone | custom fusion | bytes 2098176 | tf_op jit(solution)/shard_map/jit(_take)/gather | solution.py:70
  21.5 2.5 %gather_fusion.12 = bf16[256,4,512]{2,1,0:T(4,128)(2,1)} fusion(bf16[4,512,512]{2,0,1:T(4,128)(2,1)S(1)} %pad_maximum_fusion, s32[1024]{0:T(1024)S(1)} %pad_clamp_fusion), kind=kCustom, calls=%fused_computation.12.clone | custom fusion | bytes 2098176 | tf_op jit(solution)/shard_map/jit(_take)/gather | solution.py:70
  24.0 2.5 %gather_fusion.11 = bf16[256,4,512]{2,1,0:T(4,128)(2,1)} fusion(bf16[4,512,512]{2,0,1:T(4,128)(2,1)S(1)} %pad_maximum_fusion, s32[1024]{0:T(1024)S(1)} %pad_clamp_fusion.1), kind=kCustom, calls=%fused_computation.11.clone | custom fusion | bytes 2098176 | tf_op jit(solution)/shard_map/jit(_take)/gather | solution.py:70
  26.5 2.5 %gather_fusion.10 = bf16[256,4,512]{2,1,0:T(4,128)(2,1)} fusion(bf16[4,512,512]{2,0,1:T(4,128)(2,1)S(1)} %pad_maximum_fusion, s32[1024]{0:T(1024)S(1)} %pad_clamp_fusion.2), kind=kCustom, calls=%fused_computation.10.clone | custom fusion | bytes 2098176 | tf_op jit(solution)/shard_map/jit(_take)/gather | solution.py:70
  28.9 2.4 %gather_fusion.9 = bf16[256,4,512]{2,1,0:T(4,128)(2,1)} fusion(bf16[4,512,512]{2,0,1:T(4,128)(2,1)S(1)} %pad_maximum_fusion, s32[1024]{0:T(1024)S(1)} %pad_clamp_fusion.3), kind=kCustom, calls=%fused_computation.9.clone | custom fusion | bytes 2098176 | tf_op jit(solution)/shard_map/jit(_take)/gather | solution.py:70
  31.4 2.5 %gather_fusion.8 = bf16[256,4,512]{2,1,0:T(4,128)(2,1)} fusion(bf16[4,512,512]{2,0,1:T(4,128)(2,1)S(1)} %pad_maximum_fusion, s32[1024]{0:T(1024)S(1)} %pad_clamp_fusion.4), kind=kCustom, calls=%fused_computation.8.clone | custom fusion | bytes 2098176 | tf_op jit(solution)/shard_map/jit(_take)/gather | solution.py:70
  33.9 2.5 %gather_fusion.7 = bf16[256,4,512]{2,1,0:T(4,128)(2,1)} fusion(bf16[4,512,512]{2,0,1:T(4,128)(2,1)S(1)} %pad_maximum_fusion, s32[1024]{0:T(1024)S(1)} %pad_clamp_fusion.5), kind=kCustom, calls=%fused_computation.7.clone | custom fusion | bytes 2098176 | tf_op jit(solution)/shard_map/jit(_take)/gather | solution.py:70
  36.4 2.7 %gather_fusion.6 = bf16[256,4,512]{2,1,0:T(4,128)(2,1)} fusion(bf16[4,512,512]{2,0,1:T(4,128)(2,1)S(1)} %pad_maximum_fusion, s32[1024]{0:T(1024)S(1)} %pad_clamp_fusion.6), kind=kCustom, calls=%fused_computation.6.clone | custom fusion | bytes 2098176 | tf_op jit(solution)/shard_map/jit(_take)/gather | solution.py:70
  39.1 2.5 %gather_fusion.5 = bf16[256,4,512]{2,1,0:T(4,128)(2,1)} fusion(bf16[4,512,512]{2,0,1:T(4,128)(2,1)S(1)} %pad_maximum_fusion, s32[1024]{0:T(1024)S(1)} %pad_clamp_fusion.7), kind=kCustom, calls=%fused_computation.5.clone | custom fusion | bytes 2098176 | tf_op jit(solution)/shard_map/jit(_take)/gather | solution.py:70
  41.5 2.5 %gather_fusion.4 = bf16[256,4,512]{2,1,0:T(4,128)(2,1)} fusion(bf16[4,512,512]{2,0,1:T(4,128)(2,1)S(1)} %pad_maximum_fusion, s32[1024]{0:T(1024)S(1)} %pad_clamp_fusion.8), kind=kCustom, calls=%fused_computation.4.clone | custom fusion | bytes 2098176 | tf_op jit(solution)/shard_map/jit(_take)/gather | solution.py:70
  44.1 9.5 %fusion.7 = (f32[256]{0:T(256)S(1)}, f32[256]{0:T(256)S(1)}, f32[256]{0:T(256)S(1)}, f32[256]{0:T(256)S(1)}) fusion(bf16[256,4,512]{2,1,0:T(4,128)(2,1)} %gather_fusion.3, pred[256]{0:T(512)(128)(4,1)S(1)} %get-tuple-element.72, bf16[256,4,512]{2,1,0:T(4,128)(2,1)} %gather_fusion.2, pred[256]{0:T(512)(128)(4,1)S(1)} %get-tuple-element.73, ...), kind=kLoop, calls=%fused_computation.35 | loop fusion | flops 11009024 | bytes 5256192 | tf_op jit(solution)/shard_map/svf,svf->v/dot_general | solution.py:72
  53.7 14.7 %fusion.16 = (f32[256]{0:T(256)S(1)}, f32[256]{0:T(256)S(1)}, f32[256]{0:T(256)S(1)}, f32[256]{0:T(256)S(1)}, f32[256]{0:T(256)S(1)}, /*index=5*/f32[256]{0:T(25...) fusion(bf16[256,4,512]{2,1,0:T(4,128)(2,1)S(1)} %copy-done.1, pred[256]{0:T(512)(128)(4,1)S(1)} %get-tuple-element.76, ...), kind=kLoop, calls=%fused_computation.44 | loop fusion | flops 21493504 | bytes 10505472 | tf_op jit(solution)/shard_map/svf,svf->v/dot_general | solution.py:72
  68.5 9.0 %psum.7 = f32[256,13]{0,1:T(8,128)S(1)} all-reduce(f32[256,13]{0,1:T(8,128)S(1)} %stack.55), channel_id=1, replica_groups=mesh['vox'=16,'subj'=2] {'subj'}, use_global_device_ids=true, to_apply=%region_2.0 | all-reduce | flops 3328 | bytes 26624 | tf_op jit(solution)/shard_map/psum | solution.py:75
  77.5 1.0 fusion.61
  78.5 1.3 collective-permute-start.1
  79.8 9.8 %collective-permute-done.1 = f32[256]{0:T(256)S(1)} collective-permute-done((f32[256]{0:T(256)S(1)}, f32[256]{0:T(256)S(1)}, u32[]{:S(2)}, u32[]{:S(2)}) %collective-permute-start.1) | collective-permute-done | bytes 1056 | tf_op jit(solution)/shard_map/ppermute | solution.py:22
  89.6 7.1 %collective-permute-start.2 = (bf16[256,64]{0,1:T(8,128)(2,1)S(1)}, bf16[256,64]{0,1:T(8,128)(2,1)S(1)}, u32[]{:S(2)}, u32[]{:S(2)}) collective-permute-start(bf16[256,64]{0,1:T(8,128)(2,1)S(1)} %get-tuple-element.25), channel_id=1, source_target_pairs={{0,2},{2,4},{4,6},{6,8},{8,10},{10,12},{12,14},{14,16},{16,18},{18... | collective-permute-start | bytes 98312 | tf_op jit(solution)/shard_map/ppermute | solution.py:22
  97.1 1.3 collective-permute-start.3
  98.5 1.8 collective-permute-done.3
  101.1 2.9 %collective-permute-start.4 = (f32[64,64]{0,1:T(8,128)S(1)}, f32[64,64]{0,1:T(8,128)S(1)}, u32[]{:S(2)}, u32[]{:S(2)}) collective-permute-start(f32[64,64]{0,1:T(8,128)S(1)} %fusion.66), channel_id=1, source_target_pairs={{0,2},{2,0},{4,6},{6,4},{8,10},{10,8},{12,14},{14,12},{16,18},{18,... | collective-permute-start | bytes 49160 | tf_op jit(solution)/shard_map/ppermute | solution.py:14
  104.0 0.9 collective-permute-done.4
  104.9 2.6 %collective-permute-start.5 = (f32[64,64]{0,1:T(8,128)S(1)}, f32[64,64]{0,1:T(8,128)S(1)}, u32[]{:S(2)}, u32[]{:S(2)}) collective-permute-start(f32[64,64]{0,1:T(8,128)S(1)} %add.169), channel_id=1, source_target_pairs={{0,4},{2,6},{4,0},{6,2},{8,12},{10,14},{12,8},{14,10},{16,20},{18,... | collective-permute-start | bytes 49160 | tf_op jit(solution)/shard_map/ppermute | solution.py:14
  107.5 1.9 collective-permute-done.5
  109.4 1.7 collective-permute-start.6
  111.0 2.2 %collective-permute-done.6 = f32[64,64]{0,1:T(8,128)S(1)} collective-permute-done((f32[64,64]{0,1:T(8,128)S(1)}, f32[64,64]{0,1:T(8,128)S(1)}, u32[]{:S(2)}, u32[]{:S(2)}) %collective-permute-start.6) | collective-permute-done | bytes 16416 | tf_op jit(solution)/shard_map/ppermute | solution.py:14
  113.3 2.7 %collective-permute-start.7 = (f32[64,64]{0,1:T(8,128)S(1)}, f32[64,64]{0,1:T(8,128)S(1)}, u32[]{:S(2)}, u32[]{:S(2)}) collective-permute-start(f32[64,64]{0,1:T(8,128)S(1)} %add.171), channel_id=1, source_target_pairs={{0,16},{2,18},{4,20},{6,22},{8,24},{10,26},{12,28},{14,30},{16,0},... | collective-permute-start | bytes 49160 | tf_op jit(solution)/shard_map/ppermute | solution.py:14
  116.0 2.1 %collective-permute-done.7 = f32[64,64]{0,1:T(8,128)S(1)} collective-permute-done((f32[64,64]{0,1:T(8,128)S(1)}, f32[64,64]{0,1:T(8,128)S(1)}, u32[]{:S(2)}, u32[]{:S(2)}) %collective-permute-start.7) | collective-permute-done | bytes 16416 | tf_op jit(solution)/shard_map/ppermute | solution.py:14
  118.2 5.8 %cholesky.59 = f32[64,64]{1,0:T(8,128)S(1)} custom-call(f32[64,64]{1,0:T(8,128)S(1)} %fusion.49), custom_call_target="Cholesky" | custom-call | tf_op jit(solution)/shard_map/jit(cholesky)/cholesky | solution.py:39
  125.4 4.9 %custom-call.7 = f32[1,64,64]{1,2,0:T(8,128)S(1)} custom-call(f32[1,64,64]{2,1,0:T(8,128)S(1)} %fusion.41), custom_call_target="InvertDiagBlocksLowerTriangular" | custom-call | tf_op jit(solution)/shard_map/triangular_solve/custom-call.0 | solution.py:40
  130.6 1.3 collective-permute-start.8
  132.3 1.6 collective-permute-start.9
  133.9 3.8 %collective-permute-done.9 = bf16[256,64]{0,1:T(8,128)(2,1)S(1)} collective-permute-done((bf16[256,64]{0,1:T(8,128)(2,1)S(1)}, bf16[256,64]{0,1:T(8,128)(2,1)S(1)}, u32[]{:S(2)}, u32[]{:S(2)}) %collective-permute-start.9) | collective-permute-done | bytes 32800 | tf_op jit(solution)/shard_map/ppermute | solution.py:22
  138.5 2.7 %collective-permute-start.10 = (f32[64,64]{0,1:T(8,128)S(1)}, f32[64,64]{0,1:T(8,128)S(1)}, u32[]{:S(2)}, u32[]{:S(2)}) collective-permute-start(f32[64,64]{0,1:T(8,128)S(1)} %fusion.68), channel_id=1, source_target_pairs={{0,2},{2,0},{4,6},{6,4},{8,10},{10,8},{12,14},{14,12},{16,18},{18,... | collective-permute-start | bytes 49160 | tf_op jit(solution)/shard_map/ppermute | solution.py:14
  141.2 0.9 collective-permute-done.10
  142.1 2.0 collective-permute-start.11
  144.1 1.9 collective-permute-done.11
  146.0 1.7 collective-permute-start.12
  147.7 2.2 %collective-permute-done.12 = f32[64,64]{0,1:T(8,128)S(1)} collective-permute-done((f32[64,64]{0,1:T(8,128)S(1)}, f32[64,64]{0,1:T(8,128)S(1)}, u32[]{:S(2)}, u32[]{:S(2)}) %collective-permute-start.12) | collective-permute-done | bytes 16416 | tf_op jit(solution)/shard_map/ppermute | solution.py:14
  149.9 2.7 %collective-permute-start.13 = (f32[64,64]{0,1:T(8,128)S(1)}, f32[64,64]{0,1:T(8,128)S(1)}, u32[]{:S(2)}, u32[]{:S(2)}) collective-permute-start(f32[64,64]{0,1:T(8,128)S(1)} %add.179), channel_id=1, source_target_pairs={{0,16},{2,18},{4,20},{6,22},{8,24},{10,26},{12,28},{14,30},{16,0},... | collective-permute-start | bytes 49160 | tf_op jit(solution)/shard_map/ppermute | solution.py:14
  152.6 2.1 %collective-permute-done.13 = f32[64,64]{0,1:T(8,128)S(1)} collective-permute-done((f32[64,64]{0,1:T(8,128)S(1)}, f32[64,64]{0,1:T(8,128)S(1)}, u32[]{:S(2)}, u32[]{:S(2)}) %collective-permute-start.13) | collective-permute-done | bytes 16416 | tf_op jit(solution)/shard_map/ppermute | solution.py:14
  154.9 5.8 %cholesky.70 = f32[64,64]{1,0:T(8,128)S(1)} custom-call(f32[64,64]{1,0:T(8,128)S(1)} %fusion.47), custom_call_target="Cholesky" | custom-call | tf_op jit(solution)/shard_map/jit(cholesky)/cholesky | solution.py:39
  162.0 4.9 %custom-call.8 = f32[1,64,64]{1,2,0:T(8,128)S(1)} custom-call(f32[1,64,64]{2,1,0:T(8,128)S(1)} %fusion.42), custom_call_target="InvertDiagBlocksLowerTriangular" | custom-call | tf_op jit(solution)/shard_map/triangular_solve/custom-call.0 | solution.py:40
  167.2 1.3 collective-permute-start.14
  169.0 1.3 collective-permute-start.15
  170.3 4.0 %collective-permute-done.15 = bf16[256,64]{0,1:T(8,128)(2,1)S(1)} collective-permute-done((bf16[256,64]{0,1:T(8,128)(2,1)S(1)}, bf16[256,64]{0,1:T(8,128)(2,1)S(1)}, u32[]{:S(2)}, u32[]{:S(2)}) %collective-permute-start.15) | collective-permute-done | bytes 32800 | tf_op jit(solution)/shard_map/ppermute | solution.py:22
  175.2 2.7 %collective-permute-start.16 = (f32[64,64]{0,1:T(8,128)S(1)}, f32[64,64]{0,1:T(8,128)S(1)}, u32[]{:S(2)}, u32[]{:S(2)}) collective-permute-start(f32[64,64]{0,1:T(8,128)S(1)} %fusion.70), channel_id=1, source_target_pairs={{0,2},{2,0},{4,6},{6,4},{8,10},{10,8},{12,14},{14,12},{16,18},{18,... | collective-permute-start | bytes 49160 | tf_op jit(solution)/shard_map/ppermute | solution.py:14
  177.9 0.9 collective-permute-done.16
  178.7 2.0 collective-permute-start.17
  180.8 1.9 collective-permute-done.17
  182.7 1.6 collective-permute-start.18
  184.2 2.3 %collective-permute-done.18 = f32[64,64]{0,1:T(8,128)S(1)} collective-permute-done((f32[64,64]{0,1:T(8,128)S(1)}, f32[64,64]{0,1:T(8,128)S(1)}, u32[]{:S(2)}, u32[]{:S(2)}) %collective-permute-start.18) | collective-permute-done | bytes 16416 | tf_op jit(solution)/shard_map/ppermute | solution.py:14
  186.6 1.8 collective-permute-start.19
  188.4 3.0 %collective-permute-done.19 = f32[64,64]{0,1:T(8,128)S(1)} collective-permute-done((f32[64,64]{0,1:T(8,128)S(1)}, f32[64,64]{0,1:T(8,128)S(1)}, u32[]{:S(2)}, u32[]{:S(2)}) %collective-permute-start.19) | collective-permute-done | bytes 16416 | tf_op jit(solution)/shard_map/ppermute | solution.py:14
  191.5 5.8 %cholesky.81 = f32[64,64]{1,0:T(8,128)S(1)} custom-call(f32[64,64]{1,0:T(8,128)S(1)} %fusion.45), custom_call_target="Cholesky" | custom-call | tf_op jit(solution)/shard_map/jit(cholesky)/cholesky | solution.py:39
  198.7 4.9 %custom-call.9 = f32[1,64,64]{1,2,0:T(8,128)S(1)} custom-call(f32[1,64,64]{2,1,0:T(8,128)S(1)} %fusion.43), custom_call_target="InvertDiagBlocksLowerTriangular" | custom-call | tf_op jit(solution)/shard_map/triangular_solve/custom-call.0 | solution.py:40
  203.6 0.9 convolution_bitcast_fusion
  (125 shorter events, 11.3 us)
Async XLA Ops:
  0.0 2.2 %copy-start = (bf16[4,256,512]{2,1,0:T(8,128)(2,1)S(1)}, bf16[4,256,512]{2,1,0:T(8,128)(2,1)}, u32[]{:S(2)}) copy-start(bf16[4,256,512]{2,1,0:T(8,128)(2,1)} %param.9) | copy-start | bytes 3145732
  2.1 5.5 %copy-start.7 = (s32[256,13]{0,1:T(8,128)S(1)}, s32[256,13]{0,1:T(8,128)}, u32[]{:S(2)}) copy-start(s32[256,13]{0,1:T(8,128)} %param.11) | copy-start | bytes 39940
  5.0 5.2 %collective-permute-start = (bf16[4,256,512]{2,0,1:T(4,128)(2,1)S(1)}, bf16[4,256,512]{2,0,1:T(4,128)(2,1)S(1)}, u32[]{:S(2)}, u32[]{:S(2)}) collective-permute-start(bf16[4,256,512]{2,0,1:T(4,128)(2,1)S(1)} %fusion.3), channel_id=1, source_target_pairs={{0,2},{2,4},{4,6},{6,8},{8,10},{10,12},{12,14},{14,16},{16,18},{18... | collective-permute-start | bytes 3145736 | tf_op jit(solution)/shard_map/ppermute | solution.py:22
  44.0 9.6 %copy-start.1 = (bf16[256,4,512]{2,1,0:T(4,128)(2,1)S(1)}, bf16[256,4,512]{2,1,0:T(4,128)(2,1)}, u32[]{:S(2)}) copy-start(bf16[256,4,512]{2,1,0:T(4,128)(2,1)} %gather_fusion.12) | copy-start | bytes 3145732
  44.0 9.6 %copy-start.2 = (bf16[256,4,512]{2,1,0:T(4,128)(2,1)S(1)}, bf16[256,4,512]{2,1,0:T(4,128)(2,1)}, u32[]{:S(2)}) copy-start(bf16[256,4,512]{2,1,0:T(4,128)(2,1)} %gather_fusion.11) | copy-start | bytes 3145732
  44.0 9.6 %copy-start.3 = (bf16[256,4,512]{2,1,0:T(4,128)(2,1)S(1)}, bf16[256,4,512]{2,1,0:T(4,128)(2,1)}, u32[]{:S(2)}) copy-start(bf16[256,4,512]{2,1,0:T(4,128)(2,1)} %gather_fusion.10) | copy-start | bytes 3145732
  44.0 9.6 %copy-start.4 = (bf16[256,4,512]{2,1,0:T(4,128)(2,1)S(1)}, bf16[256,4,512]{2,1,0:T(4,128)(2,1)}, u32[]{:S(2)}) copy-start(bf16[256,4,512]{2,1,0:T(4,128)(2,1)} %gather_fusion.9) | copy-start | bytes 3145732
  44.0 9.6 %copy-start.5 = (bf16[256,4,512]{2,1,0:T(4,128)(2,1)S(1)}, bf16[256,4,512]{2,1,0:T(4,128)(2,1)}, u32[]{:S(2)}) copy-start(bf16[256,4,512]{2,1,0:T(4,128)(2,1)} %gather_fusion.8) | copy-start | bytes 3145732
  44.0 9.6 %copy-start.9 = (pred[256]{0:T(512)(128)(4,1)S(1)}, pred[256]{0:T(512)(128)(4,1)}, u32[]{:S(2)}) copy-start(pred[256]{0:T(512)(128)(4,1)} %get-tuple-element.78) | copy-start | bytes 772
  44.0 9.6 %copy-start.10 = (pred[256]{0:T(512)(128)(4,1)S(1)}, pred[256]{0:T(512)(128)(4,1)}, u32[]{:S(2)}) copy-start(pred[256]{0:T(512)(128)(4,1)} %get-tuple-element.79) | copy-start | bytes 772
  44.0 9.6 %copy-start.11 = (pred[256]{0:T(512)(128)(4,1)S(1)}, pred[256]{0:T(512)(128)(4,1)}, u32[]{:S(2)}) copy-start(pred[256]{0:T(512)(128)(4,1)} %get-tuple-element.80) | copy-start | bytes 772
  44.1 9.6 %copy-start.12 = (pred[256]{0:T(512)(128)(4,1)S(1)}, pred[256]{0:T(512)(128)(4,1)}, u32[]{:S(2)}) copy-start(pred[256]{0:T(512)(128)(4,1)} %get-tuple-element.81) | copy-start | bytes 772
  44.1 9.6 %copy-start.13 = (pred[256]{0:T(512)(128)(4,1)S(1)}, pred[256]{0:T(512)(128)(4,1)}, u32[]{:S(2)}) copy-start(pred[256]{0:T(512)(128)(4,1)} %get-tuple-element.82) | copy-start | bytes 772
  44.1 9.6 %copy-start.14 = (pred[256]{0:T(512)(128)(4,1)S(1)}, pred[256]{0:T(512)(128)(4,1)}, u32[]{:S(2)}) copy-start(pred[256]{0:T(512)(128)(4,1)} %get-tuple-element.83) | copy-start | bytes 772
  44.1 9.6 %copy-start.15 = (pred[256]{0:T(512)(128)(4,1)S(1)}, pred[256]{0:T(512)(128)(4,1)}, u32[]{:S(2)}) copy-start(pred[256]{0:T(512)(128)(4,1)} %compare_and_fusion.8) | copy-start | bytes 772
  53.7 26.1 %copy-start.8 = (s32[256]{0:T(256)S(1)}, s32[256]{0:T(256)}, u32[]{:S(2)}) copy-start(s32[256]{0:T(256)} %param.10) | copy-start | bytes 3076
  53.7 35.9 %copy-start.6 = (f32[256,64]{0,1:T(8,128)S(1)}, f32[256,64]{0,1:T(8,128)}, u32[]{:S(2)}) copy-start(f32[256,64]{0,1:T(8,128)} %param.12) | copy-start | bytes 196612
  78.5 11.1 %collective-permute-start.1 = (f32[256]{0:T(256)S(1)}, f32[256]{0:T(256)S(1)}, u32[]{:S(2)}, u32[]{:S(2)}) collective-permute-start(f32[256]{0:T(256)S(1)} %slice.190), channel_id=1, source_target_pairs={{2,0},{4,2},{6,4},{8,6},{10,8},{12,10},{14,12},{16,14},{18,16},{20... | collective-permute-start | bytes 3080 | tf_op jit(solution)/shard_map/ppermute | solution.py:22
  89.6 8.8 %collective-permute-start.2 = (bf16[256,64]{0,1:T(8,128)(2,1)S(1)}, bf16[256,64]{0,1:T(8,128)(2,1)S(1)}, u32[]{:S(2)}, u32[]{:S(2)}) collective-permute-start(bf16[256,64]{0,1:T(8,128)(2,1)S(1)} %get-tuple-element.25), channel_id=1, source_target_pairs={{0,2},{2,4},{4,6},{6,8},{8,10},{10,12},{12,14},{14,16},{16,18},{18... | collective-permute-start | bytes 98312 | tf_op jit(solution)/shard_map/ppermute | solution.py:22
  97.1 3.1 %collective-permute-start.3 = (bf16[256,64]{0,1:T(8,128)(2,1)S(1)}, bf16[256,64]{0,1:T(8,128)(2,1)S(1)}, u32[]{:S(2)}, u32[]{:S(2)}) collective-permute-start(bf16[256,64]{0,1:T(8,128)(2,1)S(1)} %slice.264), channel_id=1, source_target_pairs={{2,0},{4,2},{6,4},{8,6},{10,8},{12,10},{14,12},{16,14},{18,16},{20... | collective-permute-start | bytes 98312 | tf_op jit(solution)/shard_map/ppermute | solution.py:22
  101.1 3.8 %collective-permute-start.4 = (f32[64,64]{0,1:T(8,128)S(1)}, f32[64,64]{0,1:T(8,128)S(1)}, u32[]{:S(2)}, u32[]{:S(2)}) collective-permute-start(f32[64,64]{0,1:T(8,128)S(1)} %fusion.66), channel_id=1, source_target_pairs={{0,2},{2,0},{4,6},{6,4},{8,10},{10,8},{12,14},{14,12},{16,18},{18,... | collective-permute-start | bytes 49160 | tf_op jit(solution)/shard_map/ppermute | solution.py:14
  104.9 4.5 %collective-permute-start.5 = (f32[64,64]{0,1:T(8,128)S(1)}, f32[64,64]{0,1:T(8,128)S(1)}, u32[]{:S(2)}, u32[]{:S(2)}) collective-permute-start(f32[64,64]{0,1:T(8,128)S(1)} %add.169), channel_id=1, source_target_pairs={{0,4},{2,6},{4,0},{6,2},{8,12},{10,14},{12,8},{14,10},{16,20},{18,... | collective-permute-start | bytes 49160 | tf_op jit(solution)/shard_map/ppermute | solution.py:14
  109.4 3.9 %collective-permute-start.6 = (f32[64,64]{0,1:T(8,128)S(1)}, f32[64,64]{0,1:T(8,128)S(1)}, u32[]{:S(2)}, u32[]{:S(2)}) collective-permute-start(f32[64,64]{0,1:T(8,128)S(1)} %add.170), channel_id=1, source_target_pairs={{0,8},{2,10},{4,12},{6,14},{8,0},{10,2},{12,4},{14,6},{16,24},{18,... | collective-permute-start | bytes 49160 | tf_op jit(solution)/shard_map/ppermute | solution.py:14
  113.3 4.8 %collective-permute-start.7 = (f32[64,64]{0,1:T(8,128)S(1)}, f32[64,64]{0,1:T(8,128)S(1)}, u32[]{:S(2)}, u32[]{:S(2)}) collective-permute-start(f32[64,64]{0,1:T(8,128)S(1)} %add.171), channel_id=1, source_target_pairs={{0,16},{2,18},{4,20},{6,22},{8,24},{10,26},{12,28},{14,30},{16,0},... | collective-permute-start | bytes 49160 | tf_op jit(solution)/shard_map/ppermute | solution.py:14
  130.6 3.3 %collective-permute-start.8 = (bf16[256,64]{0,1:T(8,128)(2,1)S(1)}, bf16[256,64]{0,1:T(8,128)(2,1)S(1)}, u32[]{:S(2)}, u32[]{:S(2)}) collective-permute-start(bf16[256,64]{0,1:T(8,128)(2,1)S(1)} %get-tuple-element.23), channel_id=1, source_target_pairs={{0,2},{2,4},{4,6},{6,8},{8,10},{10,12},{12,14},{14,16},{16,18},{18... | collective-permute-start | bytes 98312 | tf_op jit(solution)/shard_map/ppermute | solution.py:22
  132.3 5.3 %collective-permute-start.9 = (bf16[256,64]{0,1:T(8,128)(2,1)S(1)}, bf16[256,64]{0,1:T(8,128)(2,1)S(1)}, u32[]{:S(2)}, u32[]{:S(2)}) collective-permute-start(bf16[256,64]{0,1:T(8,128)(2,1)S(1)} %slice.263), channel_id=1, source_target_pairs={{2,0},{4,2},{6,4},{8,6},{10,8},{12,10},{14,12},{16,14},{18,16},{20... | collective-permute-start | bytes 98312 | tf_op jit(solution)/shard_map/ppermute | solution.py:22
  138.5 3.6 %collective-permute-start.10 = (f32[64,64]{0,1:T(8,128)S(1)}, f32[64,64]{0,1:T(8,128)S(1)}, u32[]{:S(2)}, u32[]{:S(2)}) collective-permute-start(f32[64,64]{0,1:T(8,128)S(1)} %fusion.68), channel_id=1, source_target_pairs={{0,2},{2,0},{4,6},{6,4},{8,10},{10,8},{12,14},{14,12},{16,18},{18,... | collective-permute-start | bytes 49160 | tf_op jit(solution)/shard_map/ppermute | solution.py:14
  142.1 3.9 %collective-permute-start.11 = (f32[64,64]{0,1:T(8,128)S(1)}, f32[64,64]{0,1:T(8,128)S(1)}, u32[]{:S(2)}, u32[]{:S(2)}) collective-permute-start(f32[64,64]{0,1:T(8,128)S(1)} %add.177), channel_id=1, source_target_pairs={{0,4},{2,6},{4,0},{6,2},{8,12},{10,14},{12,8},{14,10},{16,20},{18,... | collective-permute-start | bytes 49160 | tf_op jit(solution)/shard_map/ppermute | solution.py:14
  146.0 3.9 %collective-permute-start.12 = (f32[64,64]{0,1:T(8,128)S(1)}, f32[64,64]{0,1:T(8,128)S(1)}, u32[]{:S(2)}, u32[]{:S(2)}) collective-permute-start(f32[64,64]{0,1:T(8,128)S(1)} %add.178), channel_id=1, source_target_pairs={{0,8},{2,10},{4,12},{6,14},{8,0},{10,2},{12,4},{14,6},{16,24},{18,... | collective-permute-start | bytes 49160 | tf_op jit(solution)/shard_map/ppermute | solution.py:14
  149.9 4.8 %collective-permute-start.13 = (f32[64,64]{0,1:T(8,128)S(1)}, f32[64,64]{0,1:T(8,128)S(1)}, u32[]{:S(2)}, u32[]{:S(2)}) collective-permute-start(f32[64,64]{0,1:T(8,128)S(1)} %add.179), channel_id=1, source_target_pairs={{0,16},{2,18},{4,20},{6,22},{8,24},{10,26},{12,28},{14,30},{16,0},... | collective-permute-start | bytes 49160 | tf_op jit(solution)/shard_map/ppermute | solution.py:14
  167.2 3.1 %collective-permute-start.14 = (bf16[256,64]{0,1:T(8,128)(2,1)S(1)}, bf16[256,64]{0,1:T(8,128)(2,1)S(1)}, u32[]{:S(2)}, u32[]{:S(2)}) collective-permute-start(bf16[256,64]{0,1:T(8,128)(2,1)S(1)} %get-tuple-element.21), channel_id=1, source_target_pairs={{0,2},{2,4},{4,6},{6,8},{8,10},{10,12},{12,14},{14,16},{16,18},{18... | collective-permute-start | bytes 98312 | tf_op jit(solution)/shard_map/ppermute | solution.py:22
  169.0 5.4 %collective-permute-start.15 = (bf16[256,64]{0,1:T(8,128)(2,1)S(1)}, bf16[256,64]{0,1:T(8,128)(2,1)S(1)}, u32[]{:S(2)}, u32[]{:S(2)}) collective-permute-start(bf16[256,64]{0,1:T(8,128)(2,1)S(1)} %slice.262), channel_id=1, source_target_pairs={{2,0},{4,2},{6,4},{8,6},{10,8},{12,10},{14,12},{16,14},{18,16},{20... | collective-permute-start | bytes 98312 | tf_op jit(solution)/shard_map/ppermute | solution.py:22
  175.2 3.6 %collective-permute-start.16 = (f32[64,64]{0,1:T(8,128)S(1)}, f32[64,64]{0,1:T(8,128)S(1)}, u32[]{:S(2)}, u32[]{:S(2)}) collective-permute-start(f32[64,64]{0,1:T(8,128)S(1)} %fusion.70), channel_id=1, source_target_pairs={{0,2},{2,0},{4,6},{6,4},{8,10},{10,8},{12,14},{14,12},{16,18},{18,... | collective-permute-start | bytes 49160 | tf_op jit(solution)/shard_map/ppermute | solution.py:14
  178.7 3.9 %collective-permute-start.17 = (f32[64,64]{0,1:T(8,128)S(1)}, f32[64,64]{0,1:T(8,128)S(1)}, u32[]{:S(2)}, u32[]{:S(2)}) collective-permute-start(f32[64,64]{0,1:T(8,128)S(1)} %add.185), channel_id=1, source_target_pairs={{0,4},{2,6},{4,0},{6,2},{8,12},{10,14},{12,8},{14,10},{16,20},{18,... | collective-permute-start | bytes 49160 | tf_op jit(solution)/shard_map/ppermute | solution.py:14
  182.7 3.9 %collective-permute-start.18 = (f32[64,64]{0,1:T(8,128)S(1)}, f32[64,64]{0,1:T(8,128)S(1)}, u32[]{:S(2)}, u32[]{:S(2)}) collective-permute-start(f32[64,64]{0,1:T(8,128)S(1)} %add.186), channel_id=1, source_target_pairs={{0,8},{2,10},{4,12},{6,14},{8,0},{10,2},{12,4},{14,6},{16,24},{18,... | collective-permute-start | bytes 49160 | tf_op jit(solution)/shard_map/ppermute | solution.py:14
  186.6 4.8 %collective-permute-start.19 = (f32[64,64]{0,1:T(8,128)S(1)}, f32[64,64]{0,1:T(8,128)S(1)}, u32[]{:S(2)}, u32[]{:S(2)}) collective-permute-start(f32[64,64]{0,1:T(8,128)S(1)} %add.187), channel_id=1, source_target_pairs={{0,16},{2,18},{4,20},{6,22},{8,24},{10,26},{12,28},{14,30},{16,0},... | collective-permute-start | bytes 49160 | tf_op jit(solution)/shard_map/ppermute | solution.py:14
